TPU v7x, 32 devices: a whole 2x2x4 slice. The times are simulated.
32 devices in a mesh: gx: 4 (over y, core), gy: 4 (over z), gz: 2 (over x).
Axes of the slice: x: 2, y: 2, z: 4, core: 2. Of those that a mesh axis runs over, the one named last changes fastest.
Arguments:
- tokens: bfloat16 [256, 7168], P(('gx', 'gy', 'gz')), may hold values from -6 to 6
- expert_ids: int32 [256, 8], P(('gx', 'gy', 'gz')), may hold values from 0 to 15, as said below
- slot_ids: int32 [256, 8], P(('gx', 'gy', 'gz')), may hold values from 0 to 7, as said below
- route_weight: bfloat16 [256, 8], P(('gx', 'gy', 'gz')), may hold values from 0.099609375 to 0.59765625
- gate_weight: bfloat16 [16, 7168, 2048], P(('gx', 'gy'), None, 'gz'), may hold values from -0.0625 to 0.0625
- up_weight: bfloat16 [16, 7168, 2048], P(('gx', 'gy'), None, 'gz'), may hold values from -0.0625 to 0.0625
- down_weight: bfloat16 [16, 2048, 7168], P(('gx', 'gy'), 'gz'), may hold values from -0.125 to 0.125
- expert_bias: float32 [16], replicated, may hold values from -3 to 3
Outputs:
- combined: bfloat16 [256, 7168], P(('gx', 'gy', 'gz'))
- expert_load: int32 [16], replicated
- new_bias: float32 [16], replicated
Inputs may be any that keep to these rules, and one draw needn't show every extreme that they name: `expert_ids`: the 8 experts of a token are different. Among the 8 tokens of one device no expert is named more than 8 times; one expert is named by every token of every device. `slot_ids`: for each device and expert, the routes of that device's tokens to that expert hold different slots.
All inputs are finite; a program needn't handle non-finite values.
Results may differ from a plain program's by a relative error of at most 0.015.
Values may be sent and summed in bfloat16 or wider, within the bound.
A program may use at most 128 MiB of HBM per device.

v0:
```python
import jax
import jax.numpy as jnp
from jax import lax
from jax.sharding import PartitionSpec as P

PLACE_LIMIT = 8
bias_rate = 0.001


def pack_rows(targets, tokens, row_total):
    selection = jnp.any(
        targets[None, :, :] == jnp.arange(row_total, dtype=jnp.int32)[:, None, None], axis=2
    )
    return jnp.dot(
        selection.astype(jnp.bfloat16), tokens, preferred_element_type=jnp.float32
    ).astype(jnp.bfloat16)


def send_rows(buffer):
    arrived = lax.all_to_all(buffer, ("gx", "gy", "gz"), split_axis=1, concat_axis=1, tiled=True)
    return arrived


def return_rows(buffer):
    arrived = lax.all_to_all(buffer, ("gx", "gy", "gz"), split_axis=1, concat_axis=1, tiled=True)
    return arrived


def body(
    tokens, expert_ids, slot_ids, route_weight, gate_weight, up_weight, down_weight, expert_bias
):
    experts = lax.axis_size("gx") * lax.axis_size("gy")
    gz_parts = lax.axis_size("gz")
    devices = experts * gz_parts
    tok_rows, model_width = tokens.shape
    route_count = expert_ids.shape[1]
    capacity = PLACE_LIMIT
    slot_share = capacity // gz_parts
    expert_index = jnp.arange(experts, dtype=jnp.int32)
    local_hits = jnp.sum((expert_ids[:, :, None] == expert_index).astype(jnp.int32), axis=(0, 1))
    expert_load = lax.psum(local_hits, ("gx", "gy", "gz"))
    mean_load = tok_rows * devices * route_count // experts
    new_bias = expert_bias + bias_rate * jnp.sign((mean_load - expert_load).astype(jnp.float32))
    back_rows = slot_ids % slot_share * devices + expert_ids * gz_parts + slot_ids // slot_share
    packed = pack_rows(slot_ids * experts + expert_ids, tokens, capacity * experts)
    repeated = jnp.broadcast_to(
        packed.reshape(capacity, experts, 1, model_width),
        (capacity, experts, gz_parts, model_width),
    )
    received = send_rows(repeated.reshape(capacity, devices, model_width))
    gate_mat = gate_weight[0]
    up_mat = up_weight[0]
    down_mat = down_weight[0]
    flat_rows = received.reshape(slot_share * lax.axis_size("gz") * devices, model_width)
    gate_act = jnp.dot(flat_rows, gate_mat, preferred_element_type=jnp.float32)
    up_act = jnp.dot(flat_rows, up_mat, preferred_element_type=jnp.float32)
    hidden = (jax.nn.silu(gate_act) * up_act).astype(jnp.bfloat16)
    partial_out = jnp.dot(hidden, down_mat, preferred_element_type=jnp.float32)
    summed = lax.psum_scatter(
        partial_out.reshape(slot_share * lax.axis_size("gz"), devices, model_width).astype(
            jnp.bfloat16
        ),
        "gz",
        scatter_dimension=0,
        tiled=True,
    )
    answers = return_rows(summed)
    flat_answers = answers.reshape(slot_share * devices, model_width)
    spread = jnp.where(
        back_rows[:, :, None] == jnp.arange(slot_share * devices, dtype=jnp.int32),
        route_weight.astype(jnp.float32)[:, :, None],
        0.0,
    )
    mixing = jnp.sum(spread, axis=1).astype(jnp.bfloat16)
    combined = jnp.dot(mixing, flat_answers, preferred_element_type=jnp.float32).astype(
        jnp.bfloat16
    )
    return (combined, expert_load, new_bias)


def solution(mesh):
    return jax.shard_map(
        body,
        mesh=mesh,
        in_specs=(
            P(("gx", "gy", "gz"), None),
            P(("gx", "gy", "gz"), None),
            P(("gx", "gy", "gz"), None),
            P(("gx", "gy", "gz"), None),
            P(("gx", "gy"), None, "gz"),
            P(("gx", "gy"), None, "gz"),
            P(("gx", "gy"), "gz", None),
            P(),
        ),
        out_specs=(P(("gx", "gy", "gz"), None), P(), P()),
        check_vma=False,
    )
```

profile of v0, /device:TPU:0, one launch (start us, length us, event | category | flops | bytes accessed | tf_op | source)
XLA Modules:
  0.0 253.8 jit_solution(9949804390127732930)
XLA Ops:
  7.2 0.0 copy-start
  7.2 0.0 reduce-scatter.2.cloned.1.call-start
  7.2 0.7 fusion.18
  7.9 0.1 fusion.15
  8.0 0.0 copy-done
  8.1 0.7 convolution_convert_fusion
  8.8 1.0 copy.17
  9.8 0.4 broadcast_in_dim.29
  10.2 0.0 copy-start.4
  10.2 90.8 %all_to_all.10 = bf16[8,32,7168]{2,0,1:T(8,128)(2,1)S(1)} all-to-all(bf16[8,32,7168]{2,0,1:T(8,128)(2,1)S(1)} %bitcast.28), channel_id=1, replica_groups=mesh['gx'=4,'gy'=4,'gz'=2] {'gx','gy','gz'}, dimensions={1} | all-to-all | bytes 7340032 | tf_op jit(solution)/shard_map/all_to_all | solution.py:20
  101.0 2.0 copy.18
  103.0 4.1 %fusion.4 = f32[256,1024]{1,0:T(8,128)S(1)} fusion(bf16[256,7168]{1,0:T(8,128)(2,1)S(1)} %bitcast.31, bf16[1,7168,1024]{2,1,0:T(8,128)(2,1)S(1)} %copy-done.4), kind=kOutput, calls=%fused_computation.4 | convolution fusion | flops 3758096384 | bytes 19398656 | tf_op jit(solution)/shard_map/dot_general | solution.py:55
  107.1 7.6 %fusion.12 = bf16[256,1024]{1,0:T(8,128)(2,1)S(1)} fusion(bf16[256,7168]{1,0:T(8,128)(2,1)S(1)} %bitcast.32, bf16[1,7168,1024]{2,1,0:T(8,128)(2,1)} %param.13, f32[256,1024]{1,0:T(8,128)S(1)} %fusion.4), kind=kOutput, calls=%fused_computation.10 | convolution fusion | flops 3759669248 | bytes 19922944 | tf_op jit(solution)/shard_map/dot_general | solution.py:56
  114.7 10.6 %fusion.6 = bf16[8,32,7168]{2,1,0:T(8,128)(2,1)} fusion(bf16[8,32,1024]{2,1,0:T(8,128)(2,1)S(1)} %bitcast.33, bf16[1,1024,7168]{2,1,0:T(8,128)(2,1)} %param.14), kind=kOutput, calls=%fused_computation.6 | convolution fusion | flops 3759931392 | bytes 18874368 | tf_op jit(solution)/shard_map/dot_general | solution.py:58
  125.3 0.0 reduce-scatter.2.cloned.1.call-update
  125.4 47.0 %reduce-scatter.2.cloned.1.call-done = bf16[4,32,7168]{2,1,0:T(8,128)(2,1)} async-done(((bf16[8,32,7168]{2,1,0:T(8,128)(2,1)}), bf16[4,32,7168]{2,1,0:T(8,128)(2,1)}) %reduce-scatter.2.cloned.1.call-update) | async-done | bytes 1835024 | tf_op jit(solution)/shard_map/reduce_scatter | solution.py:59
  172.4 4.2 %copy.19 = bf16[4,32,7168]{2,0,1:T(4,128)(2,1)} copy(bf16[4,32,7168]{2,1,0:T(8,128)(2,1)} %reduce-scatter.2.cloned.1.call-done) | data formatting | bytes 3670016 | tf_op jit(solution)/shard_map/reduce_scatter | solution.py:59
  176.6 4.6 %all-to-all-start.1 = ((bf16[4,32,7168]{2,0,1:T(4,128)(2,1)}), bf16[4,32,7168]{2,0,1:T(4,128)(2,1)S(1)}, u32[]{:S(2)}, u32[]{:S(2)}) async-start(bf16[4,32,7168]{2,0,1:T(4,128)(2,1)} %copy.19), calls=%async_computation.2 | async-start | bytes 3670016 | tf_op jit(solution)/shard_map/all_to_all | solution.py:25
  181.2 0.1 convert_reduce_fusion
  181.3 63.4 %psum.7 = s32[16]{0:T(128)S(1)} all-reduce(s32[16]{0:T(128)S(1)} %convert_reduce_fusion), channel_id=1, replica_groups=mesh['gx'=4,'gy'=4,'gz'=2] {'gx','gy','gz'}, use_global_device_ids=true, to_apply=%region_4.5 | all-reduce | flops 16 | bytes 128 | tf_op jit(solution)/shard_map/psum | solution.py:41
  244.7 0.1 select_reduce_fusion
  244.8 0.5 multiply_add_fusion.1
  245.4 0.5 copy.20
  245.9 1.0 convolution_convert_fusion.1
  (13 shorter events, 0.0 us)
Async XLA Ops:
  7.2 0.9 copy-start
  7.2 165.2 %reduce-scatter.2.cloned.1.call-start = ((), (), s32[]{:S(2)}) async-start(), calls=%async_computation.3 | async-start | bytes 5505024 | tf_op jit(solution)/shard_map/reduce_scatter | solution.py:59
  10.2 92.8 %copy-start.4 = (bf16[1,7168,1024]{2,1,0:T(8,128)(2,1)S(1)}, bf16[1,7168,1024]{2,1,0:T(8,128)(2,1)}, u32[]{:S(2)}) copy-start(bf16[1,7168,1024]{2,1,0:T(8,128)(2,1)} %param.12) | copy-start | bytes 44040196
  125.3 55.9 %copy-start.2 = (s32[8,8]{1,0:T(8,128)S(1)}, s32[8,8]{1,0:T(8,128)}, u32[]{:S(2)}) copy-start(s32[8,8]{1,0:T(8,128)} %param.9) | copy-start | bytes 772
  125.4 119.4 %copy-start.3 = (bf16[8,8]{1,0:T(8,128)(2,1)S(1)}, bf16[8,8]{1,0:T(8,128)(2,1)}, u32[]{:S(2)}) copy-start(bf16[8,8]{1,0:T(8,128)(2,1)} %param.11) | copy-start | bytes 388
  125.4 119.5 %copy-start.5 = (f32[16]{0:T(128)S(1)}, f32[16]{0:T(128)}, u32[]{:S(2)}) copy-start(f32[16]{0:T(128)} %param.15) | copy-start | bytes 196
  176.6 68.8 %all-to-all-start.1 = ((bf16[4,32,7168]{2,0,1:T(4,128)(2,1)}), bf16[4,32,7168]{2,0,1:T(4,128)(2,1)S(1)}, u32[]{:S(2)}, u32[]{:S(2)}) async-start(bf16[4,32,7168]{2,0,1:T(4,128)(2,1)} %copy.19), calls=%async_computation.2 | async-start | bytes 3670016 | tf_op jit(solution)/shard_map/all_to_all | solution.py:25
  181.2 65.7 %copy-start.1 = (bf16[8,7168]{1,0:T(8,128)(2,1)S(1)}, bf16[8,7168]{1,0:T(8,128)(2,1)}, u32[]{:S(2)}) copy-start(bf16[8,7168]{1,0:T(8,128)(2,1)} %param.8) | copy-start | bytes 344068
  244.7 2.2 copy-start.6
Sparse Core Ops, SparseCore 0:
  125.5 46.9 reduce-scatter.1
where the time goes:
time: 254 us
  blocking collectives  154 us (61%)
  waiting for transfers between devices  47.1 us (19%)
  matrix products  24 us (9%)
  between operations  14.2 us (6%)
  local copies, waits for them, and re-layouts  8.22 us (3%)
  starting transfers between devices  4.65 us (2%)
    all_to_all x1, blocking collectives, send_rows(): lax.all_to_all(buffer, ('gx', 'gy', 'gz'), split_axis=1, concat_axis=1, t...  90.8 us
    psum x1, blocking collectives, body(): expert_load = lax.psum(local_hits, ('gx', 'gy', 'gz'))  63.4 us
    reduce_scatter x1, waiting for transfers between devices, body(): lax.psum_scatter(partial_out.reshape(slot_share * lax.axis_size('gz'), de...  47 us
    dot_general x1, matrix products, body(): partial_out = jnp.dot(hidden, down_mat, preferred_element_type=jnp.float32)  10.6 us
    dot_general x1, matrix products, body(): up_act = jnp.dot(flat_rows, up_mat, preferred_element_type=jnp.float32)  7.61 us
  transfers between devices with their start and end apart: 2, of which 1 were waited for; matrix products, arithmetic and copies ran while one was open for 0% of the time, Pallas kernels for 0%

commit v1 on v0

--- a/solution.py
+++ b/solution.py
@@ -17,7 +17,15 @@
 
 
 def send_rows(buffer):
-    arrived = lax.all_to_all(buffer, ("gx", "gy", "gz"), split_axis=1, concat_axis=1, tiled=True)
+    arrived = jnp.concatenate(
+        lax.all_to_all(
+            jnp.stack(jnp.split(buffer, lax.axis_size(("gx", "gy", "gz")), axis=1)),
+            ("gx", "gy", "gz"),
+            0,
+            0,
+        ),
+        axis=1,
+    )
     return arrived
 
 

time: 254 us -> 250 us (0.984)
  matrix products: 24 us -> 19 us
    dot_general x1, matrix products: 10.6 us -> 5.53 us  [body(): partial_out = jnp.dot(hidden, down_mat, preferred_element_type=jnp.float32)]
where the time goes in v1:
time: 250 us
  blocking collectives  154 us (62%)
  waiting for transfers between devices  47.1 us (19%)
  matrix products  19 us (8%)
  between operations  14.5 us (6%)
  local copies, waits for them, and re-layouts  8.65 us (3%)
  starting transfers between devices  4.65 us (2%)
    all_to_all x1, blocking collectives, send_rows(): lax.all_to_all(jnp.stack(jnp.split(buffer, lax.axis_size(('gx', 'gy', 'gz...  90.8 us
    psum x1, blocking collectives, body(): expert_load = lax.psum(local_hits, ('gx', 'gy', 'gz'))  63.4 us
    reduce_scatter x1, waiting for transfers between devices, body(): lax.psum_scatter(partial_out.reshape(slot_share * lax.axis_size('gz'), de...  47 us
    dot_general x1, matrix products, body(): up_act = jnp.dot(flat_rows, up_mat, preferred_element_type=jnp.float32)  7.78 us
    dot_general x1, matrix products, body(): partial_out = jnp.dot(hidden, down_mat, preferred_element_type=jnp.float32)  5.53 us
  transfers between devices with their start and end apart: 2, of which 1 were waited for; matrix products, arithmetic and copies ran while one was open for 0% of the time, Pallas kernels for 0%

profile of v1, /device:TPU:0, one launch (start us, length us, event | category | flops | bytes accessed | tf_op | source)
XLA Modules:
  0.0 249.6 jit_solution(11695127239687724095)
XLA Ops:
  7.2 0.0 copy-start
  7.2 0.0 reduce-scatter.2.cloned.1.call-start
  7.2 0.7 fusion.50
  7.9 0.1 fusion.47
  8.0 0.0 copy-done
  8.1 0.7 convolution_convert_fusion
  8.8 1.0 copy.51
  9.8 0.5 broadcast_in_dim.29
  10.8 0.0 slice-start.2
  10.9 90.8 %all_to_all.10 = bf16[32,8,1,7168]{3,1,2,0:T(8,128)(2,1)S(1)} all-to-all(bf16[32,8,1,7168]{3,1,2,0:T(8,128)(2,1)S(1)} %fusion.15), channel_id=1, replica_groups=mesh['gx'=4,'gy'=4,'gz'=2] {'gx','gy','gz'}, dimensions={0} | all-to-all | bytes 7340032 | tf_op jit(solution)/shard_map/all_to_all | solution.py:21
  101.6 2.0 copy.52
  103.7 4.0 %fusion.4 = f32[256,1024]{1,0:T(8,128)S(1)} fusion(bf16[256,7168]{1,0:T(8,128)(2,1)S(1)} %bitcast.192, bf16[1,7168,1024]{2,1,0:T(8,128)(2,1)S(1)} %bitcast.195), kind=kOutput, calls=%fused_computation.4 | convolution fusion | flops 3758096384 | bytes 19398656 | tf_op jit(solution)/shard_map/dot_general | solution.py:63
  107.8 7.8 %fusion.12 = bf16[256,1024]{1,0:T(8,128)(2,1)S(1)} fusion(bf16[256,7168]{1,0:T(8,128)(2,1)S(1)} %bitcast.193, bf16[1,7168,1024]{2,1,0:T(8,128)(2,1)} %param.13, f32[256,1024]{1,0:T(8,128)S(1)} %fusion.4), kind=kOutput, calls=%fused_computation.10 | convolution fusion | flops 3759669248 | bytes 19922944 | tf_op jit(solution)/shard_map/dot_general | solution.py:64
  115.6 5.5 %fusion.6 = bf16[8,32,7168]{2,1,0:T(8,128)(2,1)} fusion(bf16[8,32,1024]{2,1,0:T(8,128)(2,1)S(1)} %bitcast.198, bf16[1,1024,7168]{2,1,0:T(8,128)(2,1)S(1)} %bitcast.197), kind=kOutput, calls=%fused_computation.6 | convolution fusion | flops 3759931392 | bytes 18874368 | tf_op jit(solution)/shard_map/dot_general | solution.py:66
  121.2 0.0 reduce-scatter.2.cloned.1.call-update
  121.2 47.0 %reduce-scatter.2.cloned.1.call-done = bf16[4,32,7168]{2,1,0:T(8,128)(2,1)} async-done(((bf16[8,32,7168]{2,1,0:T(8,128)(2,1)}), bf16[4,32,7168]{2,1,0:T(8,128)(2,1)}) %reduce-scatter.2.cloned.1.call-update) | async-done | bytes 1835024 | tf_op jit(solution)/shard_map/reduce_scatter | solution.py:67
  168.3 4.2 %copy.53 = bf16[4,32,7168]{2,0,1:T(4,128)(2,1)} copy(bf16[4,32,7168]{2,1,0:T(8,128)(2,1)} %reduce-scatter.2.cloned.1.call-done) | data formatting | bytes 3670016 | tf_op jit(solution)/shard_map/reduce_scatter | solution.py:67
  172.5 4.6 %all-to-all-start.1 = ((bf16[4,32,7168]{2,0,1:T(4,128)(2,1)}), bf16[4,32,7168]{2,0,1:T(4,128)(2,1)S(1)}, u32[]{:S(2)}, u32[]{:S(2)}) async-start(bf16[4,32,7168]{2,0,1:T(4,128)(2,1)} %copy.53), calls=%async_computation.2 | async-start | bytes 3670016 | tf_op jit(solution)/shard_map/all_to_all | solution.py:33
  177.1 0.1 convert_reduce_fusion
  177.2 63.4 %psum.7 = s32[16]{0:T(128)S(1)} all-reduce(s32[16]{0:T(128)S(1)} %convert_reduce_fusion), channel_id=1, replica_groups=mesh['gx'=4,'gy'=4,'gz'=2] {'gx','gy','gz'}, use_global_device_ids=true, to_apply=%region_4.5 | all-reduce | flops 16 | bytes 128 | tf_op jit(solution)/shard_map/psum | solution.py:49
  240.6 0.1 select_reduce_fusion
  240.7 0.5 multiply_add_fusion.1
  241.2 0.5 copy.54
  241.8 1.0 convolution_convert_fusion.1
  (61 shorter events, 0.4 us)
Async XLA Ops:
  7.2 0.9 copy-start
  7.2 161.1 %reduce-scatter.2.cloned.1.call-start = ((), (), s32[]{:S(2)}) async-start(), calls=%async_computation.3 | async-start | bytes 5505024 | tf_op jit(solution)/shard_map/reduce_scatter | solution.py:67
  8.8 94.9 %slice-start = ((s8[14680064]{0:T(1024)(128)(4,1)}), s8[4194304]{0:T(1024)(128)(4,1)S(1)}, s32[]{:S(2)}) async-start(s8[14680064]{0:T(1024)(128)(4,1)} %bitcast.194), calls=%async_computation.4 | async-start | bytes 8388608
  9.8 93.9 %slice-start.1 = ((s8[14680064]{0:T(1024)(128)(4,1)}), s8[4194304]{0:T(1024)(128)(4,1)S(1)}, s32[]{:S(2)}) async-start(s8[14680064]{0:T(1024)(128)(4,1)} %bitcast.194), calls=%async_computation.5 | async-start | bytes 8388608
  10.8 92.9 %slice-start.2 = ((s8[14680064]{0:T(1024)(128)(4,1)}), s8[4194304]{0:T(1024)(128)(4,1)S(1)}, s32[]{:S(2)}) async-start(s8[14680064]{0:T(1024)(128)(4,1)} %bitcast.194), calls=%async_computation.6 | async-start | bytes 8388608
  10.9 92.8 %slice-start.3 = ((s8[14680064]{0:T(1024)(128)(4,1)}), s8[2097152]{0:T(1024)(128)(4,1)S(1)}, s32[]{:S(2)}) async-start(s8[14680064]{0:T(1024)(128)(4,1)} %bitcast.194), calls=%async_computation.7 | async-start | bytes 4194304
  103.7 11.9 %slice-start.4 = ((s8[14680064]{0:T(1024)(128)(4,1)}), s8[2097152]{0:T(1024)(128)(4,1)S(1)}, s32[]{:S(2)}) async-start(s8[14680064]{0:T(1024)(128)(4,1)} %bitcast.196), calls=%async_computation.8 | async-start | bytes 4194304
  103.7 11.9 %slice-start.5 = ((s8[14680064]{0:T(1024)(128)(4,1)}), s8[4194304]{0:T(1024)(128)(4,1)S(1)}, s32[]{:S(2)}) async-start(s8[14680064]{0:T(1024)(128)(4,1)} %bitcast.196), calls=%async_computation.9 | async-start | bytes 8388608
  107.8 7.8 %slice-start.6 = ((s8[14680064]{0:T(1024)(128)(4,1)}), s8[4194304]{0:T(1024)(128)(4,1)S(1)}, s32[]{:S(2)}) async-start(s8[14680064]{0:T(1024)(128)(4,1)} %bitcast.196), calls=%async_computation.10 | async-start | bytes 8388608
  107.8 7.8 %slice-start.7 = ((s8[14680064]{0:T(1024)(128)(4,1)}), s8[4194304]{0:T(1024)(128)(4,1)S(1)}, s32[]{:S(2)}) async-start(s8[14680064]{0:T(1024)(128)(4,1)} %bitcast.196), calls=%async_computation.11 | async-start | bytes 8388608
  121.2 55.9 %copy-start.2 = (s32[8,8]{1,0:T(8,128)S(1)}, s32[8,8]{1,0:T(8,128)}, u32[]{:S(2)}) copy-start(s32[8,8]{1,0:T(8,128)} %param.9) | copy-start | bytes 772
  121.2 119.4 %copy-start.3 = (bf16[8,8]{1,0:T(8,128)(2,1)S(1)}, bf16[8,8]{1,0:T(8,128)(2,1)}, u32[]{:S(2)}) copy-start(bf16[8,8]{1,0:T(8,128)(2,1)} %param.11) | copy-start | bytes 388
  121.2 119.5 %copy-start.4 = (f32[16]{0:T(128)S(1)}, f32[16]{0:T(128)}, u32[]{:S(2)}) copy-start(f32[16]{0:T(128)} %param.15) | copy-start | bytes 196
  172.5 68.8 %all-to-all-start.1 = ((bf16[4,32,7168]{2,0,1:T(4,128)(2,1)}), bf16[4,32,7168]{2,0,1:T(4,128)(2,1)S(1)}, u32[]{:S(2)}, u32[]{:S(2)}) async-start(bf16[4,32,7168]{2,0,1:T(4,128)(2,1)} %copy.53), calls=%async_computation.2 | async-start | bytes 3670016 | tf_op jit(solution)/shard_map/all_to_all | solution.py:33
  177.1 65.7 %copy-start.1 = (bf16[8,7168]{1,0:T(8,128)(2,1)S(1)}, bf16[8,7168]{1,0:T(8,128)(2,1)}, u32[]{:S(2)}) copy-start(bf16[8,7168]{1,0:T(8,128)(2,1)} %param.8) | copy-start | bytes 344068
  240.6 2.2 copy-start.5
Sparse Core Ops, SparseCore 0:
  121.3 46.9 reduce-scatter.1
